TPU v7x, 32 devices: a whole 2x2x4 slice. The times are simulated.
32 devices in a mesh: shard: 4 (over y, x), replica: 8 (over z, core).
Axes of the slice: x: 2, y: 2, z: 4, core: 2. Of those that a mesh axis runs over, the one named last changes fastest.
Arguments:
- tokens: bfloat16 [8192, 1536], P(('shard', 'replica')), may hold values from -6 to 6
- cotangent: bfloat16 [8192, 1536], P(('shard', 'replica')), may hold values from -6 to 6
- seq_lengths: int32 [64], replicated, may hold values from 0 to 256, as said below
- seq_device: int32 [64], replicated, may hold values from 0 to 31
- seq_offsets: int32 [64], replicated, may hold values from 0 to 1
- norm_attn: bfloat16 [1, 1536], P(None, 'shard'), may hold values from 0.5 to 1.5
- w_qkv: bfloat16 [1, 1536, 3072], P(None, 'shard'), may hold values from -0.15625 to 0.15625
- w_out: bfloat16 [1, 1536, 1536], P(None, 'shard'), may hold values from -0.625 to 0.625
- norm_mlp: bfloat16 [1, 1536], P(None, 'shard'), may hold values from 0.5 to 1.5
- w_gate_up: bfloat16 [1, 1536, 8192], P(None, 'shard'), may hold values from -0.15625 to 0.15625
- w_down: bfloat16 [1, 4096, 1536], P(None, 'shard'), may hold values from -0.125 to 0.125
Outputs:
- result: bfloat16 [8192, 1536], P(('shard', 'replica'))
- grad_tokens: float32 [8192, 1536], P(('shard', 'replica'))
- grad_norm_attn: float32 [1, 1536], P(None, 'shard')
- grad_w_qkv: float32 [1, 1536, 3072], P(None, 'shard')
- grad_w_out: float32 [1, 1536, 1536], P(None, 'shard')
- grad_norm_mlp: float32 [1, 1536], P(None, 'shard')
- grad_w_gate_up: float32 [1, 1536, 8192], P(None, 'shard')
- grad_w_down: float32 [1, 4096, 1536], P(None, 'shard')
Inputs may be any that keep to these rules, and one draw needn't show every extreme that they name: `seq_lengths`: each device is named by exactly 2 entries. A sequence lies within blocks 2p and 2p + 1 of its device for some p; sequences of one device never share a row; length 0 marks an unused entry. In every draw some device is full, its every pair of blocks holding one sequence of length 256.
All inputs are finite; a program needn't handle non-finite values.
Results may differ from a plain program's by a relative error of at most 0.02.
Values may be sent and summed in bfloat16 or wider, within the bound.
A program may use at most 320 MiB of HBM per device.

v0:
```python
import jax
import jax.numpy as jnp
from jax import lax
from jax.sharding import PartitionSpec as P

HEADS = 16
KV_HEADS = 8
HEAD = 96
FF = 4096
BLOCK = 128
epsilon = 1e-05
rope_base = 100000.0


def rms_scale(field):
    return lax.rsqrt(jnp.mean(field * field, axis=-1, keepdims=True) + epsilon)


def rotate(field):
    half = field.shape[-1] // 2
    return jnp.concatenate([-field[..., half:], field[..., :half]], axis=-1)


def rope_tables(position):
    half = HEAD // 2
    freqs = rope_base ** (-(jnp.arange(half, dtype=jnp.float32) * 2.0) / HEAD)
    angles = position.astype(jnp.float32)[:, None] * freqs[None, :]
    cosine = jnp.cos(angles)
    sine = jnp.sin(angles)
    return (jnp.concatenate([cosine, cosine], axis=-1), jnp.concatenate([sine, sine], axis=-1))


def locate(device, seq_lengths, seq_device, seq_offsets, rows):
    starts = seq_offsets * BLOCK
    local = jnp.arange(rows, dtype=jnp.int32)
    labels = jnp.arange(seq_lengths.shape[0], dtype=jnp.int32)
    hits = (
        (seq_device[None, :] == device)
        & (local[:, None] >= starts[None, :])
        & (local[:, None] < (starts + seq_lengths)[None, :])
    )
    segment = jnp.max(jnp.where(hits, labels[None, :], -1), axis=1)
    begin = jnp.sum(jnp.where(hits, starts[None, :], 0), axis=1)
    return (segment, local - begin)


def mask_of(segment):
    local = jnp.arange(segment.shape[0], dtype=jnp.int32)
    return (segment[:, None] == segment[None, :]) & (local[None, :] <= local[:, None])


def contract_rows(left, right):
    return lax.dot_general(
        left, right, (((0,), (0,)), ((), ())), preferred_element_type=jnp.float32
    )


def contract_cols(left, right):
    return lax.dot_general(
        left, right, (((1,), (1,)), ((), ())), preferred_element_type=jnp.float32
    )


def norm_rows(field, gain):
    scale = rms_scale(field)
    normed = (field * scale * gain.astype(jnp.float32)[None, :]).astype(jnp.bfloat16)
    return (scale, normed)


def norm_back(grad_normed, field, scale, gain):
    normed = field * scale
    grad_gain = jnp.sum(grad_normed * normed, axis=0)
    inner = grad_normed * gain[None, :]
    grad_field = scale * (inner - normed * jnp.mean(inner * normed, axis=-1, keepdims=True))
    return (grad_field, grad_gain)


def split_project(project, q_heads, k_heads, cosine, sine):
    rows = project.shape[0]
    width_q = q_heads * HEAD
    width_k = k_heads * HEAD
    queries = project[:, :width_q].reshape(rows, q_heads, HEAD)
    keys = project[:, width_q : width_q + width_k].reshape(rows, k_heads, HEAD)
    values_b = project[:, width_q + width_k :].reshape(rows, k_heads, HEAD).astype(jnp.bfloat16)
    queries_b = (queries * cosine[:, None, :] + rotate(queries) * sine[:, None, :]).astype(
        jnp.bfloat16
    )
    keys_b = (keys * cosine[:, None, :] + rotate(keys) * sine[:, None, :]).astype(jnp.bfloat16)
    return (queries_b, keys_b, values_b)


def join_grads(grad_queries, grad_keys, grad_values, cosine, sine):
    rows = grad_queries.shape[0]
    grad_queries = grad_queries * cosine[:, None, :] - rotate(grad_queries * sine[:, None, :])
    grad_keys = grad_keys * cosine[:, None, :] - rotate(grad_keys * sine[:, None, :])
    return jnp.concatenate(
        [
            grad_queries.reshape(rows, -1),
            grad_keys.reshape(rows, -1),
            grad_values.reshape(rows, -1),
        ],
        axis=1,
    ).astype(jnp.bfloat16)


def attention_scores(queries_b, keys_b, allowed):
    rows = queries_b.shape[0]
    kv_count = keys_b.shape[1]
    grouped = queries_b.reshape(rows, kv_count, queries_b.shape[1] // kv_count, HEAD)
    scores = jnp.einsum(
        "qkgd,pkd->kgqp", grouped, keys_b, preferred_element_type=jnp.float32
    ) * HEAD ** (-0.5)
    return jnp.where(allowed, scores, -1e30)


def attend_forward(queries_b, keys_b, values_b, allowed):
    rows = queries_b.shape[0]
    scores = attention_scores(queries_b, keys_b, allowed)
    top = jnp.max(scores, axis=-1, keepdims=True)
    total = jnp.log(jnp.sum(jnp.exp(scores - top), axis=-1, keepdims=True)) + top
    weights_b = jnp.exp(scores - total).astype(jnp.bfloat16)
    mixed = jnp.einsum("kgqp,pkd->qkgd", weights_b, values_b, preferred_element_type=jnp.float32)
    return (mixed.reshape(rows, -1).astype(jnp.bfloat16), total)


def attend_backward(grad_mixed_b, queries_b, keys_b, values_b, total, allowed):
    rows = queries_b.shape[0]
    q_heads = queries_b.shape[1]
    kv_count = keys_b.shape[1]
    per = q_heads // kv_count
    factor = HEAD ** (-0.5)
    grad_mixed = grad_mixed_b.reshape(rows, kv_count, per, HEAD)
    weights = jnp.exp(attention_scores(queries_b, keys_b, allowed) - total)
    weights_b = weights.astype(jnp.bfloat16)
    grad_values = jnp.einsum(
        "kgqp,qkgd->pkd", weights_b, grad_mixed, preferred_element_type=jnp.float32
    )
    grad_weights = jnp.einsum(
        "qkgd,pkd->kgqp", grad_mixed, values_b, preferred_element_type=jnp.float32
    )
    grad_scores = weights * (grad_weights - jnp.sum(weights * grad_weights, axis=-1, keepdims=True))
    grad_scores_b = grad_scores.astype(jnp.bfloat16)
    grouped = queries_b.reshape(rows, kv_count, per, HEAD)
    grad_queries = jnp.einsum(
        "kgqp,pkd->qkgd", grad_scores_b, keys_b, preferred_element_type=jnp.float32
    )
    grad_queries = grad_queries.reshape(rows, q_heads, HEAD) * factor
    grad_keys = (
        jnp.einsum("kgqp,qkgd->pkd", grad_scores_b, grouped, preferred_element_type=jnp.float32)
        * factor
    )
    return (grad_queries, grad_keys, grad_values)


def gate_back(grad_hidden, gate_up, local_ff):
    gate = gate_up[:, :local_ff]
    upper = gate_up[:, local_ff:]
    sigma = jax.nn.sigmoid(gate)
    grad_gate = grad_hidden * upper * sigma * (1.0 + gate * (1.0 - sigma))
    grad_upper = grad_hidden * (gate * sigma)
    return jnp.concatenate([grad_gate, grad_upper], axis=1).astype(jnp.bfloat16)


def attention_forward(field, gain, w_project, w_output, allowed, cosine, sine):
    scale, normed = norm_rows(field, gain)
    project = jnp.dot(normed, w_project, preferred_element_type=jnp.float32)
    queries_b, keys_b, values_b = split_project(project, HEADS, KV_HEADS, cosine, sine)
    mixed, total = attend_forward(queries_b, keys_b, values_b, allowed)
    after = field + jnp.dot(mixed, w_output, preferred_element_type=jnp.float32)
    return (after, (scale, normed, queries_b, keys_b, values_b, total, mixed))


def attention_backward(grad_field, field, gain, w_project, w_output, saved, allowed, cosine, sine):
    scale, normed, queries_b, keys_b, values_b, total, mixed = saved
    grad_branch = grad_field.astype(jnp.bfloat16)
    grad_w_output = contract_rows(mixed, grad_branch)
    grad_mixed = contract_cols(grad_branch, w_output).astype(jnp.bfloat16)
    grad_queries, grad_keys, grad_values = attend_backward(
        grad_mixed, queries_b, keys_b, values_b, total, allowed
    )
    grad_project = join_grads(grad_queries, grad_keys, grad_values, cosine, sine)
    grad_w_project = contract_rows(normed, grad_project)
    grad_normed = contract_cols(grad_project, w_project)
    grad_input, grad_gain = norm_back(grad_normed, field, scale, gain.astype(jnp.float32))
    return (grad_field + grad_input, grad_gain, grad_w_project, grad_w_output)


def mlp_forward(field, gain, w_gateup, w_lower):
    scale, normed = norm_rows(field, gain)
    gate_up = jnp.dot(normed, w_gateup, preferred_element_type=jnp.float32)
    hidden = (jax.nn.silu(gate_up[:, :FF]) * gate_up[:, FF:]).astype(jnp.bfloat16)
    after = field + jnp.dot(hidden, w_lower, preferred_element_type=jnp.float32)
    return (after, (scale, normed, gate_up, hidden))


def mlp_backward(grad_field, field, gain, w_gateup, w_lower, saved):
    scale, normed, gate_up, hidden = saved
    grad_branch = grad_field.astype(jnp.bfloat16)
    grad_w_lower = contract_rows(hidden, grad_branch)
    grad_hidden = contract_cols(grad_branch, w_lower)
    grad_gateup = gate_back(grad_hidden, gate_up, FF)
    grad_w_gateup = contract_rows(normed, grad_gateup)
    grad_normed = contract_cols(grad_gateup, w_gateup)
    grad_input, grad_gain = norm_back(grad_normed, field, scale, gain.astype(jnp.float32))
    return (grad_field + grad_input, grad_gain, grad_w_gateup, grad_w_lower)


def settle(owned):
    return (
        lax.psum(owned[0].astype(jnp.bfloat16), "replica").astype(jnp.float32),
        lax.psum(owned[1].astype(jnp.bfloat16), "replica").astype(jnp.float32),
        lax.psum(owned[2].astype(jnp.bfloat16), "replica").astype(jnp.float32),
        lax.psum(owned[3].astype(jnp.bfloat16), "replica").astype(jnp.float32),
        lax.psum(owned[4].astype(jnp.bfloat16), "replica").astype(jnp.float32),
        lax.psum(owned[5].astype(jnp.bfloat16), "replica").astype(jnp.float32),
    )


def body(
    tokens,
    cotangent,
    seq_lengths,
    seq_device,
    seq_offsets,
    norm_attn,
    w_qkv,
    w_out,
    norm_mlp,
    w_gate_up,
    w_down,
):
    rows = tokens.shape[0]
    layers = w_qkv.shape[0]
    device = lax.axis_index(("shard", "replica"))
    segment, position = locate(device, seq_lengths, seq_device, seq_offsets, rows)
    live = (segment >= 0).astype(jnp.float32)[:, None]
    field = tokens.astype(jnp.float32)
    per_layer = [None] * layers
    cosine, sine = rope_tables(position)
    allowed = mask_of(segment)
    layer = 0
    attn_parts = (
        lax.all_gather(norm_attn[layer], "shard", axis=0, tiled=True),
        lax.all_gather(w_qkv[layer], "shard", axis=0, tiled=True),
        lax.all_gather(w_out[layer], "shard", axis=0, tiled=True),
    )
    middle, attn_saved = attention_forward(
        field, attn_parts[0], attn_parts[1], attn_parts[2], allowed, cosine, sine
    )
    mlp_parts = (
        lax.all_gather(norm_mlp[layer], "shard", axis=0, tiled=True),
        lax.all_gather(w_gate_up[layer], "shard", axis=0, tiled=True),
        lax.all_gather(w_down[layer], "shard", axis=0, tiled=True),
    )
    after, mlp_saved = mlp_forward(middle, mlp_parts[0], mlp_parts[1], mlp_parts[2])
    kept_inputs = [(field, attn_saved, middle, mlp_saved)]
    result = (after * live).astype(jnp.bfloat16)
    grad_field = cotangent.astype(jnp.float32) * live
    for layer in reversed(range(layers)):
        field_in, attn_saved, middle, mlp_saved = kept_inputs[layer]
        mlp_parts = (
            lax.all_gather(norm_mlp[layer], "shard", axis=0, tiled=True),
            lax.all_gather(w_gate_up[layer], "shard", axis=0, tiled=True),
            lax.all_gather(w_down[layer], "shard", axis=0, tiled=True),
        )
        grad_middle, grad_gain_mlp, grad_gateup, grad_lower = mlp_backward(
            grad_field, middle, mlp_parts[0], mlp_parts[1], mlp_parts[2], mlp_saved
        )
        mlp_owned = (
            lax.psum_scatter(
                grad_gain_mlp.astype(jnp.bfloat16), "shard", scatter_dimension=0, tiled=True
            ).astype(jnp.float32),
            lax.psum_scatter(
                grad_gateup.astype(jnp.bfloat16), "shard", scatter_dimension=0, tiled=True
            ).astype(jnp.float32),
            lax.psum_scatter(
                grad_lower.astype(jnp.bfloat16), "shard", scatter_dimension=0, tiled=True
            ).astype(jnp.float32),
        )
        attn_parts = (
            lax.all_gather(norm_attn[layer], "shard", axis=0, tiled=True),
            lax.all_gather(w_qkv[layer], "shard", axis=0, tiled=True),
            lax.all_gather(w_out[layer], "shard", axis=0, tiled=True),
        )
        grad_field, grad_gain_attn, grad_project, grad_output = attention_backward(
            grad_middle,
            field_in,
            attn_parts[0],
            attn_parts[1],
            attn_parts[2],
            attn_saved,
            allowed,
            cosine,
            sine,
        )
        attn_owned = (
            lax.psum_scatter(
                grad_gain_attn.astype(jnp.bfloat16), "shard", scatter_dimension=0, tiled=True
            ).astype(jnp.float32),
            lax.psum_scatter(
                grad_project.astype(jnp.bfloat16), "shard", scatter_dimension=0, tiled=True
            ).astype(jnp.float32),
            lax.psum_scatter(
                grad_output.astype(jnp.bfloat16), "shard", scatter_dimension=0, tiled=True
            ).astype(jnp.float32),
        )
        per_layer[layer] = settle(
            (attn_owned[0], attn_owned[1], attn_owned[2], mlp_owned[0], mlp_owned[1], mlp_owned[2])
        )
    stacked = [jnp.stack([entry[member] for entry in per_layer], axis=0) for member in range(6)]
    return (
        result,
        grad_field,
        stacked[0],
        stacked[1],
        stacked[2],
        stacked[3],
        stacked[4],
        stacked[5],
    )


def solution(mesh):
    placed = (
        P(("shard", "replica"), None),
        P(("shard", "replica"), None),
        P(),
        P(),
        P(),
        P(None, "shard"),
        P(None, "shard", None),
        P(None, "shard", None),
        P(None, "shard"),
        P(None, "shard", None),
        P(None, "shard", None),
    )
    return jax.shard_map(
        body,
        mesh=mesh,
        in_specs=placed,
        out_specs=(
            P(("shard", "replica"), None),
            P(("shard", "replica"), None),
            P(None, "shard"),
            P(None, "shard", None),
            P(None, "shard", None),
            P(None, "shard"),
            P(None, "shard", None),
            P(None, "shard", None),
        ),
        check_vma=False,
    )
```

profile of v0, /device:TPU:0, one launch (start us, length us, event | category | flops | bytes accessed | tf_op | source)
XLA Modules:
  0.0 1345.5 jit_solution(480248952729375393)
XLA Ops:
  10.1 9.6 all-gather
  19.7 8.2 all-gather.3
  28.4 0.7 broadcast_multiply_fusion.1
  30.7 78.1 %all-gather.11.cloned.1.call-done = bf16[1,1536,3072]{2,1,0:T(8,128)(2,1)} async-done(((bf16[1,384,3072]{2,1,0:T(8,128)(2,1)}), bf16[1,1536,3072]{2,1,0:T(8,128)(2,1)}) %all-gather.11.cloned.1.call-update) | async-done | bytes 9437200 | tf_op jit(solution)/shard_map/all_gather | solution.py:244
  108.8 5.2 fusion.10
  114.1 1.3 slice.59
  115.4 0.9 copy.51
  116.6 2.1 copy.53
  118.7 1.1 fusion.57
  120.0 0.8 copy-done.22
  121.2 0.9 fusion.40
  122.1 0.9 exponential_reduce_fusion
  123.1 1.1 copy-done
  124.1 1.1 convolution_convert_fusion.4
  125.3 42.3 %all-gather.13.cloned.1.call-done = bf16[1,1536,1536]{2,1,0:T(8,128)(2,1)} async-done(((bf16[1,384,1536]{2,1,0:T(8,128)(2,1)}), bf16[1,1536,1536]{2,1,0:T(8,128)(2,1)}) %all-gather.13.cloned.1.call-update) | async-done | bytes 4718608 | tf_op jit(solution)/shard_map/all_gather | solution.py:245
  167.6 3.8 multiply_reduce_fusion.2
  171.4 225.6 %all-gather.15.cloned.1.call-done = bf16[1,1536,8192]{2,1,0:T(8,128)(2,1)} async-done(((bf16[1,384,8192]{2,1,0:T(8,128)(2,1)}), bf16[1,1536,8192]{2,1,0:T(8,128)(2,1)}) %all-gather.15.cloned.1.call-update) | async-done | bytes 25165840 | tf_op jit(solution)/shard_map/all_gather | solution.py:252
  397.1 13.8 %fusion.2 = f32[256,8192]{1,0:T(8,128)} fusion(bf16[1,1536,8192]{2,1,0:T(8,128)(2,1)} %all-gather.15.cloned.1.call-done, f32[256,1536]{1,0:T(8,128)S(1)} %get-tuple-element.44, f32[1536]{0:T(1024)S(1)} %convert_reduce_fusion, f32[256]{0:T(256)S(1)} %add_rsqrt_fusion), kind=kOutput, calls=%fused_computation.3 | convolution fusion | flops 6443630592 | bytes 35134464 | tf_op jit(solution)/shard_map/dot_general | solution.py:190
  410.9 110.3 %all-gather.17.cloned.1.call-done = bf16[1,4096,1536]{2,1,0:T(8,128)(2,1)} async-done(((bf16[1,1024,1536]{2,1,0:T(8,128)(2,1)}), bf16[1,4096,1536]{2,1,0:T(8,128)(2,1)}) %all-gather.17.cloned.1.call-update) | async-done | bytes 12582928 | tf_op jit(solution)/shard_map/all_gather | solution.py:253
  521.2 10.4 multiply_convert_fusion.1
  531.6 14.9 %multiply_reduce_fusion = (bf16[1536]{0:T(1024)(128)(2,1)}, f32[256]{0:T(256)S(1)}, f32[256,1536]{1,0:T(8,128)}) fusion(f32[256,1536]{1,0:T(8,128)S(1)} %get-tuple-element.44, f32[256]{0:T(256)S(1)} %add_rsqrt_fusion, f32[1536]{0:T(1024)S(1)} %convert_reduce_fusion, bf16[1,1536,8192]{2,1,0:T(8,128)(2,1)} %all-gather.15.cloned.1.call-done, ...), kind=kOutput, calls=%fused_computation.63 | convolution fusion | flops 6453196800 | bytes 32517120 | tf_op jit(solution)/shard_map/dot_general | solution.py:59
  546.5 2.0 multiply_add_fusion
  548.5 3.6 convolution_convert_fusion.3
  552.2 4.6 fusion.33
  556.8 2.3 copy.56
  559.1 4.2 fusion.16
  563.3 1.2 fusion.18
  565.9 0.8 copy-done.20
  567.0 0.8 broadcast_multiply_fusion
  568.1 0.9 copy-done.12
  569.0 1.1 fusion.53
  570.9 7.3 convolution_convert_fusion.2
  578.3 10.2 convolution_convert_fusion.1
  588.5 14.2 %convolution_convert_fusion = bf16[1536,8192]{1,0:T(8,128)(2,1)} fusion(bf16[256,4096]{1,0:T(8,128)(2,1)} %copy-done.16, bf16[256,4096]{1,0:T(8,128)(2,1)} %copy-done.15, f32[256,1536]{1,0:T(8,128)S(1)} %get-tuple-element.44, f32[1536]{0:T(1024)S(1)} %convert_reduce_fusion, f32[256]{0:T(256)} %copy-done.27), kind=kOutput, calls=%fused_computation | convolution fusion | flops 6464602112 | bytes 30940160 | tf_op jit(solution)/shard_map/dot_general | solution.py:53
  603.0 6.2 reduce-scatter.7.cloned.1.call-done
  609.2 97.9 %reduce-scatter.5.cloned.1.call-done = bf16[384,3072]{1,0:T(8,128)(2,1)} async-done(((bf16[1536,3072]{1,0:T(8,128)(2,1)}), bf16[384,3072]{1,0:T(8,128)(2,1)}) %reduce-scatter.5.cloned.1.call-update) | async-done | bytes 2359312 | tf_op jit(solution)/shard_map/reduce_scatter | solution.py:300
  707.1 124.3 %reduce-scatter.11.cloned.1.call-done = bf16[1024,1536]{1,0:T(8,128)(2,1)} async-done(((bf16[4096,1536]{1,0:T(8,128)(2,1)}), bf16[1024,1536]{1,0:T(8,128)(2,1)}) %reduce-scatter.11.cloned.1.call-update) | async-done | bytes 3145744 | tf_op jit(solution)/shard_map/reduce_scatter | solution.py:276
  831.4 224.9 %reduce-scatter.9.cloned.1.call-done = bf16[384,8192]{1,0:T(8,128)(2,1)} async-done(((bf16[1536,8192]{1,0:T(8,128)(2,1)}), bf16[384,8192]{1,0:T(8,128)(2,1)}) %reduce-scatter.9.cloned.1.call-update) | async-done | bytes 6291472 | tf_op jit(solution)/shard_map/reduce_scatter | solution.py:273
  1058.2 8.8 fusion.46
  1067.0 9.2 all-reduce.4
  1076.4 15.4 %all-reduce.2 = (bf16[1,384]{1,0:T(2,128)(2,1)S(1)}, bf16[1,384]{1,0:T(2,128)(2,1)S(1)}) all-reduce(bf16[1,384]{1,0:T(2,128)(2,1)S(1)} %stack.36, bf16[1,384]{1,0:T(2,128)(2,1)S(1)} %stack.42), channel_id=1, replica_groups=mesh['shard'=4,'replica'=8] {'replica'}, use_global_device_ids=true, to_apply=%region_11.12 | all-reduce | flops 768 | bytes 3072 | tf_op jit(solution)/shard_map/psum | solution.py:210
  1093.6 3.4 fusion.45
  1096.9 9.0 fusion.30
  1105.9 215.4 %all-reduce.7.cloned.1.call-done = (bf16[1,384,3072]{2,1,0:T(8,128)(2,1)}, bf16[1,384,1536]{2,1,0:T(8,128)(2,1)}, bf16[1,384,8192]{2,1,0:T(8,128)(2,1)}, bf16[1,1024,1536]{2,1,0:T(8,128)(2,1)}) async-done(((bf16[1,384,3072]{2,1,0:T(8,128)(2,1)}, bf16[1,384,1536]{2,1,0:T(8,128)(2,1)}, bf16[1,384,8192]{2,1,0:T(8,128)(2,1)}, bf16[1,1024,1536]{2,1,0:T(8,128)(2,1)}), (bf16[1,384,3072]{2,1,0:T(8,128)(2,1)}, ...) | async-done | bytes 12976144 | tf_op jit(solution)/shard_map/psum | solution.py:211
  1321.3 4.6 stack.39
  1325.9 3.0 stack.41
  1328.8 6.3 stack.45
  1335.2 3.6 stack.47
  (132 shorter events, 12.1 us)
Async XLA Ops:
  7.2 101.6 %all-gather.11.cloned.1.call-start = ((), (), s32[]{:S(2)}) async-start(), calls=%async_computation.8 | async-start | bytes 11796480 | tf_op jit(solution)/shard_map/all_gather | solution.py:244
  7.9 159.7 %all-gather.13.cloned.1.call-start = ((), (), s32[]{:S(2)}) async-start(), calls=%async_computation.9 | async-start | bytes 5898240 | tf_op jit(solution)/shard_map/all_gather | solution.py:245
  8.7 388.4 %all-gather.15.cloned.1.call-start = ((), (), s32[]{:S(2)}) async-start(), calls=%async_computation.10 | async-start | bytes 31457280 | tf_op jit(solution)/shard_map/all_gather | solution.py:252
  9.4 10.3 copy-start.36
  9.4 18.5 %copy-start.39 = (s32[64]{0:T(128)S(1)}, s32[64]{0:T(128)}, u32[]{:S(2)}) copy-start(s32[64]{0:T(128)} %param.14) | copy-start | bytes 772
  9.4 18.6 %copy-start.37 = (s32[64]{0:T(128)S(1)}, s32[64]{0:T(128)}, u32[]{:S(2)}) copy-start(s32[64]{0:T(128)} %param.15) | copy-start | bytes 772
  9.4 18.6 %copy-start.38 = (s32[64]{0:T(128)S(1)}, s32[64]{0:T(128)}, u32[]{:S(2)}) copy-start(s32[64]{0:T(128)} %param.13) | copy-start | bytes 772
  9.4 19.7 %copy-start.2 = (bf16[256,1536]{1,0:T(8,128)(2,1)S(1)}, bf16[256,1536]{1,0:T(8,128)(2,1)}, u32[]{:S(2)}) copy-start(bf16[256,1536]{1,0:T(8,128)(2,1)} %param.11) | copy-start | bytes 2359300
  9.4 511.8 %all-gather.17.cloned.1.call-start = ((), (), s32[]{:S(2)}) async-start(), calls=%async_computation.11 | async-start | bytes 15728640 | tf_op jit(solution)/shard_map/all_gather | solution.py:253
  10.0 599.2 %reduce-scatter.7.cloned.1.call-start = ((), (), s32[]{:S(2)}) async-start(), calls=%async_computation.5 | async-start | bytes 5898240 | tf_op jit(solution)/shard_map/reduce_scatter | solution.py:303
  29.4 84.6 %copy-start.28 = (f32[256]{0:T(256)}, f32[256]{0:T(256)S(1)}, u32[]{:S(2)}) copy-start(f32[256]{0:T(256)S(1)} %add_rsqrt_fusion.1) | copy-start | bytes 3076
  119.9 0.9 copy-start.22
  119.9 1.0 copy-start.23
  120.0 1.2 copy-start.17
  121.2 0.9 copy-start.6
  122.1 2.0 copy-start
  122.1 2.0 copy-start.19
  123.1 2.2 copy-start.25
  125.3 46.1 %copy-start.4 = (bf16[8,96,2,256]{3,1,2,0:T(8,128)(2,1)}, bf16[8,96,2,256]{3,1,2,0:T(8,128)(2,1)S(1)}, u32[]{:S(2)}) copy-start(bf16[8,96,2,256]{3,1,2,0:T(8,128)(2,1)S(1)} %convolution_convert_fusion.4) | copy-start | bytes 2359300
  171.4 360.2 %copy-start.27 = (f32[256]{0:T(256)}, f32[256]{0:T(256)S(1)}, u32[]{:S(2)}) copy-start(f32[256]{0:T(256)S(1)} %add_rsqrt_fusion) | copy-start | bytes 3076
  397.1 124.1 %copy-start.10 = (bf16[256,1536]{1,0:T(8,128)(2,1)S(1)}, bf16[256,1536]{1,0:T(8,128)(2,1)}, u32[]{:S(2)}) copy-start(bf16[256,1536]{1,0:T(8,128)(2,1)} %param.12) | copy-start | bytes 2359300
  397.1 124.1 %copy-start.31 = (f32[256]{0:T(256)S(1)}, f32[256]{0:T(256)}, u32[]{:S(2)}) copy-start(f32[256]{0:T(256)} %compare_convert_fusion) | copy-start | bytes 3076
  531.6 14.9 %copy-start.15 = (bf16[256,4096]{1,0:T(8,128)(2,1)}, bf16[256,4096]{1,0:T(8,128)(2,1)S(1)}, u32[]{:S(2)}) copy-start(bf16[256,4096]{1,0:T(8,128)(2,1)S(1)} %get-tuple-element.22) | copy-start | bytes 6291460
  531.6 14.9 %copy-start.16 = (bf16[256,4096]{1,0:T(8,128)(2,1)}, bf16[256,4096]{1,0:T(8,128)(2,1)S(1)}, u32[]{:S(2)}) copy-start(bf16[256,4096]{1,0:T(8,128)(2,1)S(1)} %get-tuple-element.23) | copy-start | bytes 6291460
  531.6 14.9 %copy-start.11 = (bf16[256,1536]{1,0:T(8,128)(2,1)S(1)}, bf16[256,1536]{1,0:T(8,128)(2,1)}, u32[]{:S(2)}) copy-start(bf16[256,1536]{1,0:T(8,128)(2,1)} %param.12) | copy-start | bytes 2359300
  531.6 14.9 %copy-start.32 = (f32[256]{0:T(256)S(1)}, f32[256]{0:T(256)}, u32[]{:S(2)}) copy-start(f32[256]{0:T(256)} %compare_convert_fusion) | copy-start | bytes 3076
  546.5 2.0 copy-start.5
  552.1 155.0 %reduce-scatter.5.cloned.1.call-start = ((), (), s32[]{:S(2)}) async-start(), calls=%async_computation.4 | async-start | bytes 11796480 | tf_op jit(solution)/shard_map/reduce_scatter | solution.py:300
  559.1 4.2 copy-start.1
  559.1 4.2 copy-start.18
  559.1 4.2 copy-start.26
  564.6 0.9 copy-start.21
  565.7 0.9 copy-start.20
  565.9 1.2 copy-start.7
  567.0 3.1 copy-start.14
  567.8 1.1 copy-start.12
  568.9 1.9 copy-start.3
  569.0 1.9 copy-start.29
  570.1 0.7 copy-start.24
  578.2 253.2 %reduce-scatter.11.cloned.1.call-start = ((), (), s32[]{:S(2)}) async-start(), calls=%async_computation.7 | async-start | bytes 15728640 | tf_op jit(solution)/shard_map/reduce_scatter | solution.py:276
  588.5 467.8 %reduce-scatter.9.cloned.1.call-start = ((), (), s32[]{:S(2)}) async-start(), calls=%async_computation.6 | async-start | bytes 31457280 | tf_op jit(solution)/shard_map/reduce_scatter | solution.py:273
  602.8 718.6 %all-reduce.7.cloned.1.call-start = ((), (), s32[]{:S(2)}) async-start(), calls=%async_computation.12 | async-start | bytes 25952256 | tf_op jit(solution)/shard_map/psum | solution.py:211
  1056.3 1.9 copy-start.30
  1058.2 8.8 copy-start.34
  1093.6 3.4 copy-start.9
  1093.6 3.4 copy-start.33
  1321.3 7.5 copy-start.8
  1328.8 6.3 copy-start.13
  (2 other events, 1.3 us)
Sparse Core Ops, SparseCore 0:
  9.8 98.9 all-gather.10
  110.6 56.9 all-gather.12
  169.5 227.5 all-gather.14
  398.8 122.4 all-gather.16
  552.3 56.9 reduce-scatter.6
  612.2 94.8 reduce-scatter.4
  710.8 120.5 reduce-scatter.10
  834.5 221.7 reduce-scatter.8
  1058.9 262.3 all-reduce.6
where the time goes:
time: 1350 us
  waiting for transfers between devices  1130 us (84%)
  matrix products  114 us (8%)
  blocking collectives  42.4 us (3%)
  other arithmetic  32 us (2%)
  between operations  15.3 us (1%)
    all_gather x1, waiting for transfers between devices, body(): lax.all_gather(w_gate_up[layer], 'shard', axis=0, tiled=True)  226 us
    reduce_scatter x1, waiting for transfers between devices, body(): lax.psum_scatter(grad_gateup.astype(jnp.bfloat16), 'shard', scatter_dimen...  225 us
    psum x1, waiting for transfers between devices, settle(): lax.psum(owned[1].astype(jnp.bfloat16), 'replica').astype(jnp.float32)  215 us
    reduce_scatter x1, waiting for transfers between devices, body(): lax.psum_scatter(grad_lower.astype(jnp.bfloat16), 'shard', scatter_dimens...  124 us
    all_gather x1, waiting for transfers between devices, body(): lax.all_gather(w_down[layer], 'shard', axis=0, tiled=True)  110 us
    reduce_scatter x1, waiting for transfers between devices, body(): lax.psum_scatter(grad_project.astype(jnp.bfloat16), 'shard', scatter_dime...  97.9 us
    all_gather x1, waiting for transfers between devices, body(): lax.all_gather(w_qkv[layer], 'shard', axis=0, tiled=True)  78.1 us
    all_gather x1, waiting for transfers between devices, body(): lax.all_gather(w_out[layer], 'shard', axis=0, tiled=True)  42.3 us
  transfers between devices with their start and end apart: 9, of which 9 were waited for; matrix products, arithmetic and copies ran while one was open for 8% of the time, Pallas kernels for 0%

commit v1 on v0

--- a/solution.py
+++ b/solution.py
@@ -10,6 +10,24 @@
 BLOCK = 128
 epsilon = 1e-05
 rope_base = 100000.0
+
+
+def collect(shard, axis, dim):
+    ways, here, hop = (lax.axis_size(axis), lax.axis_index(axis), shard.shape[dim])
+    shape = [n * ways if d == dim else n for d, n in enumerate(shard.shape)]
+    full = lax.dynamic_update_slice_in_dim(
+        jnp.zeros(shape, shard.dtype), shard, here * hop, axis=dim
+    )
+    going_up = going_down = shard
+    for far in range(1, ways // 2 + 1):
+        going_up = lax.ppermute(going_up, axis, [(d, (d + 1) % ways) for d in range(ways)])
+        full = lax.dynamic_update_slice_in_dim(full, going_up, (here - far) % ways * hop, axis=dim)
+        if 2 * far < ways:
+            going_down = lax.ppermute(going_down, axis, [(d, (d - 1) % ways) for d in range(ways)])
+            full = lax.dynamic_update_slice_in_dim(
+                full, going_down, (here + far) % ways * hop, axis=dim
+            )
+    return full
 
 
 def rms_scale(field):
@@ -250,7 +268,7 @@
     mlp_parts = (
         lax.all_gather(norm_mlp[layer], "shard", axis=0, tiled=True),
         lax.all_gather(w_gate_up[layer], "shard", axis=0, tiled=True),
-        lax.all_gather(w_down[layer], "shard", axis=0, tiled=True),
+        collect(w_down[layer], "shard", 0),
     )
     after, mlp_saved = mlp_forward(middle, mlp_parts[0], mlp_parts[1], mlp_parts[2])
     kept_inputs = [(field, attn_saved, middle, mlp_saved)]

time: 1350 us -> 1460 us (1.081)
  waiting for transfers between devices: 1130 us -> 1220 us
  local copies, waits for them, and re-layouts: 13.2 us -> 33.7 us
    reduce_scatter x1, waiting for transfers between devices: 97.9 us -> 175 us  [body(): lax.psum_scatter(grad_project.astype(jnp.bfloat16), 'shard', scatter_dime...]
    psum x1, waiting for transfers between devices: 215 us -> 148 us  [settle(): lax.psum(owned[1].astype(jnp.bfloat16), 'replica').astype(jnp.float32)]
    ppermute x0 -> x3, waiting for transfers between devices: none -> 51.8 us  [the longest x2 51.8 us: collect(): lax.ppermute(going_up, axis, [(d, (d + 1) % ways) for d in range(ways)])]
    reduce_scatter x1, waiting for transfers between devices: 124 us -> 156 us  [body(): lax.psum_scatter(grad_lower.astype(jnp.bfloat16), 'shard', scatter_dimens...]
  transfers between devices with their start and end apart: 9 -> 12, of which waited for: 9 -> 10; matrix products, arithmetic and copies ran while one was open for 8% -> 9% of each run, Pallas kernels for 0% -> 0%
where the time goes in v1:
time: 1460 us
  waiting for transfers between devices  1220 us (84%)
  matrix products  110 us (8%)
  blocking collectives  40.7 us (3%)
  local copies, waits for them, and re-layouts  33.7 us (2%)
  other arithmetic  31.9 us (2%)
  between operations  15.3 us (1%)
    all_gather x1, waiting for transfers between devices, body(): lax.all_gather(w_gate_up[layer], 'shard', axis=0, tiled=True)  226 us
    reduce_scatter x1, waiting for transfers between devices, body(): lax.psum_scatter(grad_gateup.astype(jnp.bfloat16), 'shard', scatter_dimen...  225 us
    reduce_scatter x1, waiting for transfers between devices, body(): lax.psum_scatter(grad_project.astype(jnp.bfloat16), 'shard', scatter_dime...  175 us
    reduce_scatter x1, waiting for transfers between devices, body(): lax.psum_scatter(grad_lower.astype(jnp.bfloat16), 'shard', scatter_dimens...  156 us
    psum x1, waiting for transfers between devices, settle(): lax.psum(owned[1].astype(jnp.bfloat16), 'replica').astype(jnp.float32)  148 us
    all_gather x1, waiting for transfers between devices, body(): lax.all_gather(w_down[layer], 'shard', axis=0, tiled=True)  110 us
    all_gather x1, waiting for transfers between devices, body(): lax.all_gather(w_qkv[layer], 'shard', axis=0, tiled=True)  78.1 us
    ppermute x2, waiting for transfers between devices, collect(): lax.ppermute(going_up, axis, [(d, (d + 1) % ways) for d in range(ways)])  51.8 us
  transfers between devices with their start and end apart: 12, of which 10 were waited for; matrix products, arithmetic and copies ran while one was open for 9% of the time, Pallas kernels for 0%

profile of v1, /device:TPU:0, one launch (start us, length us, event | category | flops | bytes accessed | tf_op | source)
XLA Modules:
  0.0 1455.3 jit_solution(10181029838207990703)
XLA Ops:
  10.1 9.6 all-gather
  19.7 8.2 all-gather.3
  30.7 78.1 %all-gather.11.cloned.1.call-done = bf16[1,1536,3072]{2,1,0:T(8,128)(2,1)} async-done(((bf16[1,384,3072]{2,1,0:T(8,128)(2,1)}), bf16[1,1536,3072]{2,1,0:T(8,128)(2,1)}) %all-gather.11.cloned.1.call-update) | async-done | bytes 9437200 | tf_op jit(solution)/shard_map/all_gather | solution.py:262
  108.8 5.2 fusion.8
  114.0 1.3 slice.59
  116.3 2.1 copy.53
  118.4 1.5 copy.52
  125.7 1.1 convolution_convert_fusion.4
  126.8 40.8 %all-gather.13.cloned.1.call-done = bf16[1,1536,1536]{2,1,0:T(8,128)(2,1)} async-done(((bf16[1,384,1536]{2,1,0:T(8,128)(2,1)}), bf16[1,1536,1536]{2,1,0:T(8,128)(2,1)}) %all-gather.13.cloned.1.call-update) | async-done | bytes 4718608 | tf_op jit(solution)/shard_map/all_gather | solution.py:263
  167.6 3.8 multiply_reduce_fusion.2
  171.5 225.6 %all-gather.15.cloned.1.call-done = bf16[1,1536,8192]{2,1,0:T(8,128)(2,1)} async-done(((bf16[1,384,8192]{2,1,0:T(8,128)(2,1)}), bf16[1,1536,8192]{2,1,0:T(8,128)(2,1)}) %all-gather.15.cloned.1.call-update) | async-done | bytes 25165840 | tf_op jit(solution)/shard_map/all_gather | solution.py:270
  397.1 13.8 fusion.2
  410.9 110.3 %all-gather.17.cloned.1.call-done = bf16[1,4096,1536]{2,1,0:T(8,128)(2,1)} async-done(((bf16[1,1024,1536]{2,1,0:T(8,128)(2,1)}), bf16[1,4096,1536]{2,1,0:T(8,128)(2,1)}) %all-gather.17.cloned.1.call-update) | async-done | bytes 12582928 | tf_op jit(solution)/shard_map/all_gather | solution.py:282
  521.2 10.4 multiply_convert_fusion.1
  531.6 14.9 %multiply_reduce_fusion = (bf16[1536]{0:T(1024)(128)(2,1)}, f32[256]{0:T(256)S(1)}, f32[256,1536]{1,0:T(8,128)}) fusion(f32[256,1536]{1,0:T(8,128)S(1)} %get-tuple-element.44, f32[256]{0:T(256)S(1)} %add_rsqrt_fusion, f32[1536]{0:T(1024)S(1)} %convert_reduce_fusion, bf16[1,1536,8192]{2,1,0:T(8,128)(2,1)} %all-gather.15.cloned.1.call-done, ...), kind=kOutput, calls=%fused_computation.61 | convolution fusion | flops 6453196800 | bytes 32517120 | tf_op jit(solution)/shard_map/dot_general | solution.py:77
  546.5 2.0 multiply_add_fusion
  548.5 3.6 convolution_convert_fusion.3
  552.2 4.6 fusion.24
  556.8 2.3 copy.56
  559.1 4.2 fusion.14
  563.3 1.2 fusion.16
  568.4 1.1 fusion.44
  570.3 7.3 convolution_convert_fusion.2
  577.6 10.3 convolution_convert_fusion.1
  588.0 14.2 convolution_convert_fusion
  602.2 1.6 collective-permute-start
  603.8 1.4 collective-permute-start.1
  605.2 5.5 reduce-scatter.7.cloned.1.call-done
  610.7 174.9 %reduce-scatter.5.cloned.1.call-done = bf16[384,3072]{1,0:T(8,128)(2,1)} async-done(((bf16[1536,3072]{1,0:T(8,128)(2,1)}), bf16[384,3072]{1,0:T(8,128)(2,1)}) %reduce-scatter.5.cloned.1.call-update) | async-done | bytes 2359312 | tf_op jit(solution)/shard_map/reduce_scatter | solution.py:318
  785.6 155.7 %reduce-scatter.11.cloned.1.call-done = bf16[1024,1536]{1,0:T(8,128)(2,1)} async-done(((bf16[4096,1536]{1,0:T(8,128)(2,1)}), bf16[1024,1536]{1,0:T(8,128)(2,1)}) %reduce-scatter.11.cloned.1.call-update) | async-done | bytes 3145744 | tf_op jit(solution)/shard_map/reduce_scatter | solution.py:294
  941.3 224.8 %reduce-scatter.9.cloned.1.call-done = bf16[384,8192]{1,0:T(8,128)(2,1)} async-done(((bf16[1536,8192]{1,0:T(8,128)(2,1)}), bf16[384,8192]{1,0:T(8,128)(2,1)}) %reduce-scatter.9.cloned.1.call-update) | async-done | bytes 6291472 | tf_op jit(solution)/shard_map/reduce_scatter | solution.py:291
  1166.2 1.7 collective-permute-start.2
  1169.2 6.1 broadcast_in_dim.35
  1175.3 1.9 constant_dynamic-update-slice_fusion.3
  1177.2 4.4 constant_dynamic-update-slice_fusion.2
  1181.6 4.0 constant_dynamic-update-slice_fusion.1
  1185.6 51.8 %collective-permute-done.2 = bf16[1024,1536]{1,0:T(8,128)(2,1)} collective-permute-done((bf16[1024,1536]{1,0:T(8,128)(2,1)}, bf16[1024,1536]{1,0:T(8,128)(2,1)}, u32[]{:S(2)}, u32[]{:S(2)}) %collective-permute-start.2) | collective-permute-done | bytes 3145760 | tf_op jit(solution)/shard_map/ppermute | solution.py:23
  1237.4 3.8 constant_dynamic-update-slice_fusion
  1241.2 4.7 fusion.37
  1245.9 8.4 all-reduce.4
  1254.5 14.5 all-reduce.2
  1270.8 3.3 fusion.36
  1274.0 9.0 fusion.23
  1283.0 148.2 %all-reduce.7.cloned.1.call-done = (bf16[1,384,3072]{2,1,0:T(8,128)(2,1)}, bf16[1,384,1536]{2,1,0:T(8,128)(2,1)}, bf16[1,384,8192]{2,1,0:T(8,128)(2,1)}, bf16[1,1024,1536]{2,1,0:T(8,128)(2,1)}) async-done(((bf16[1,384,3072]{2,1,0:T(8,128)(2,1)}, bf16[1,384,1536]{2,1,0:T(8,128)(2,1)}, bf16[1,384,8192]{2,1,0:T(8,128)(2,1)}, bf16[1,1024,1536]{2,1,0:T(8,128)(2,1)}), (bf16[1,384,3072]{2,1,0:T(8,128)(2,1)}, ...) | async-done | bytes 12976144 | tf_op jit(solution)/shard_map/psum | solution.py:229
  1431.2 9.3 stack.45
  1440.5 3.6 stack.47
  1444.1 2.8 stack.39
  1446.8 1.7 stack.41
  (158 shorter events, 19.7 us)
Async XLA Ops:
  7.2 101.6 %all-gather.11.cloned.1.call-start = ((), (), s32[]{:S(2)}) async-start(), calls=%async_computation.8 | async-start | bytes 11796480 | tf_op jit(solution)/shard_map/all_gather | solution.py:262
  7.9 159.7 %all-gather.13.cloned.1.call-start = ((), (), s32[]{:S(2)}) async-start(), calls=%async_computation.9 | async-start | bytes 5898240 | tf_op jit(solution)/shard_map/all_gather | solution.py:263
  8.7 388.4 %all-gather.15.cloned.1.call-start = ((), (), s32[]{:S(2)}) async-start(), calls=%async_computation.10 | async-start | bytes 31457280 | tf_op jit(solution)/shard_map/all_gather | solution.py:270
  9.4 10.3 copy-start.40
  9.4 18.5 %copy-start.43 = (s32[64]{0:T(128)S(1)}, s32[64]{0:T(128)}, u32[]{:S(2)}) copy-start(s32[64]{0:T(128)} %param.14) | copy-start | bytes 772
  9.4 18.6 %copy-start.41 = (s32[64]{0:T(128)S(1)}, s32[64]{0:T(128)}, u32[]{:S(2)}) copy-start(s32[64]{0:T(128)} %param.15) | copy-start | bytes 772
  9.4 18.6 %copy-start.42 = (s32[64]{0:T(128)S(1)}, s32[64]{0:T(128)}, u32[]{:S(2)}) copy-start(s32[64]{0:T(128)} %param.13) | copy-start | bytes 772
  9.4 19.7 %copy-start.2 = (bf16[256,1536]{1,0:T(8,128)(2,1)S(1)}, bf16[256,1536]{1,0:T(8,128)(2,1)}, u32[]{:S(2)}) copy-start(bf16[256,1536]{1,0:T(8,128)(2,1)} %param.11) | copy-start | bytes 2359300
  9.4 511.8 %all-gather.17.cloned.1.call-start = ((), (), s32[]{:S(2)}) async-start(), calls=%async_computation.11 | async-start | bytes 15728640 | tf_op jit(solution)/shard_map/all_gather | solution.py:282
  10.0 600.7 %reduce-scatter.7.cloned.1.call-start = ((), (), s32[]{:S(2)}) async-start(), calls=%async_computation.5 | async-start | bytes 5898240 | tf_op jit(solution)/shard_map/reduce_scatter | solution.py:321
  29.4 84.6 %copy-start.33 = (f32[256]{0:T(256)}, f32[256]{0:T(256)S(1)}, u32[]{:S(2)}) copy-start(f32[256]{0:T(256)S(1)} %add_rsqrt_fusion.1) | copy-start | bytes 3076
  123.7 2.0 copy-start
  123.7 2.0 copy-start.22
  124.6 43.0 %copy-start.30 = (f32[2,8,256]{2,1,0:T(8,128)}, f32[2,8,256]{2,1,0:T(8,128)S(1)}, u32[]{:S(2)}) copy-start(f32[2,8,256]{2,1,0:T(8,128)S(1)} %log_add_fusion) | copy-start | bytes 49156
  126.8 44.6 %copy-start.6 = (bf16[8,96,2,256]{3,1,2,0:T(8,128)(2,1)}, bf16[8,96,2,256]{3,1,2,0:T(8,128)(2,1)S(1)}, u32[]{:S(2)}) copy-start(bf16[8,96,2,256]{3,1,2,0:T(8,128)(2,1)S(1)} %convolution_convert_fusion.4) | copy-start | bytes 2359300
  171.4 360.2 %copy-start.32 = (f32[256]{0:T(256)}, f32[256]{0:T(256)S(1)}, u32[]{:S(2)}) copy-start(f32[256]{0:T(256)S(1)} %add_rsqrt_fusion) | copy-start | bytes 3076
  397.1 124.1 %copy-start.11 = (bf16[256,1536]{1,0:T(8,128)(2,1)S(1)}, bf16[256,1536]{1,0:T(8,128)(2,1)}, u32[]{:S(2)}) copy-start(bf16[256,1536]{1,0:T(8,128)(2,1)} %param.12) | copy-start | bytes 2359300
  397.1 124.2 %copy-start.36 = (f32[256]{0:T(256)S(1)}, f32[256]{0:T(256)}, u32[]{:S(2)}) copy-start(f32[256]{0:T(256)} %compare_convert_fusion) | copy-start | bytes 3076
  531.6 14.9 %copy-start.18 = (bf16[256,4096]{1,0:T(8,128)(2,1)}, bf16[256,4096]{1,0:T(8,128)(2,1)S(1)}, u32[]{:S(2)}) copy-start(bf16[256,4096]{1,0:T(8,128)(2,1)S(1)} %get-tuple-element.22) | copy-start | bytes 6291460
  531.6 14.9 %copy-start.19 = (bf16[256,4096]{1,0:T(8,128)(2,1)}, bf16[256,4096]{1,0:T(8,128)(2,1)S(1)}, u32[]{:S(2)}) copy-start(bf16[256,4096]{1,0:T(8,128)(2,1)S(1)} %get-tuple-element.23) | copy-start | bytes 6291460
  531.6 14.9 %copy-start.12 = (bf16[256,1536]{1,0:T(8,128)(2,1)S(1)}, bf16[256,1536]{1,0:T(8,128)(2,1)}, u32[]{:S(2)}) copy-start(bf16[256,1536]{1,0:T(8,128)(2,1)} %param.12) | copy-start | bytes 2359300
  531.6 14.9 %copy-start.37 = (f32[256]{0:T(256)S(1)}, f32[256]{0:T(256)}, u32[]{:S(2)}) copy-start(f32[256]{0:T(256)} %compare_convert_fusion) | copy-start | bytes 3076
  546.5 2.0 copy-start.7
  552.1 233.5 %reduce-scatter.5.cloned.1.call-start = ((), (), s32[]{:S(2)}) async-start(), calls=%async_computation.4 | async-start | bytes 11796480 | tf_op jit(solution)/shard_map/reduce_scatter | solution.py:318
  559.1 4.2 copy-start.1
  559.1 4.2 copy-start.21
  559.1 4.2 copy-start.31
  566.9 2.6 copy-start.15
  568.4 1.9 copy-start.34
  577.6 363.8 %reduce-scatter.11.cloned.1.call-start = ((), (), s32[]{:S(2)}) async-start(), calls=%async_computation.7 | async-start | bytes 15728640 | tf_op jit(solution)/shard_map/reduce_scatter | solution.py:294
  587.9 578.3 %reduce-scatter.9.cloned.1.call-start = ((), (), s32[]{:S(2)}) async-start(), calls=%async_computation.6 | async-start | bytes 31457280 | tf_op jit(solution)/shard_map/reduce_scatter | solution.py:291
  602.2 829.0 %all-reduce.7.cloned.1.call-start = ((), (), s32[]{:S(2)}) async-start(), calls=%async_computation.12 | async-start | bytes 25952256 | tf_op jit(solution)/shard_map/psum | solution.py:229
  602.2 564.0 %collective-permute-start = (bf16[1024,1536]{1,0:T(8,128)(2,1)}, bf16[1024,1536]{1,0:T(8,128)(2,1)}, u32[]{:S(2)}, u32[]{:S(2)}) collective-permute-start(bf16[1024,1536]{1,0:T(8,128)(2,1)} %bitcast.127), channel_id=1, source_target_pairs={{0,8},{8,16},{16,24},{24,0},{1,9},{9,17},{17,25},{25,1},{2,10},{10... | collective-permute-start | bytes 9437192 | tf_op jit(solution)/shard_map/ppermute | solution.py:23
  603.8 577.8 %collective-permute-start.1 = (bf16[1024,1536]{1,0:T(8,128)(2,1)}, bf16[1024,1536]{1,0:T(8,128)(2,1)}, u32[]{:S(2)}, u32[]{:S(2)}) collective-permute-start(bf16[1024,1536]{1,0:T(8,128)(2,1)} %bitcast.128), channel_id=1, source_target_pairs={{0,24},{8,0},{16,8},{24,16},{1,25},{9,1},{17,9},{25,17},{2,26},{10... | collective-permute-start | bytes 9437192 | tf_op jit(solution)/shard_map/ppermute | solution.py:26
  1166.2 71.2 %collective-permute-start.2 = (bf16[1024,1536]{1,0:T(8,128)(2,1)}, bf16[1024,1536]{1,0:T(8,128)(2,1)}, u32[]{:S(2)}, u32[]{:S(2)}) collective-permute-start(bf16[1024,1536]{1,0:T(8,128)(2,1)} %collective-permute-done), channel_id=1, source_target_pairs={{0,8},{8,16},{16,24},{24,0},{1,9},{9,17},{17,25},{25,1},{2,10},{10... | collective-permute-start | bytes 9437192 | tf_op jit(solution)/shard_map/ppermute | solution.py:23
  1169.2 6.1 copy-start.5
  1175.3 65.8 %slice-start = ((s8[9437184]{0:T(1024)(128)(4,1)}), s8[4194304]{0:T(1024)(128)(4,1)S(1)}, s32[]{:S(2)}) async-start(s8[9437184]{0:T(1024)(128)(4,1)} %bitcast.153), calls=%async_computation.13 | async-start | bytes 8388608
  1177.2 63.9 %slice-start.1 = ((s8[9437184]{0:T(1024)(128)(4,1)}), s8[4194304]{0:T(1024)(128)(4,1)S(1)}, s32[]{:S(2)}) async-start(s8[9437184]{0:T(1024)(128)(4,1)} %bitcast.153), calls=%async_computation.14 | async-start | bytes 8388608
  1181.6 59.5 %slice-start.2 = ((s8[9437184]{0:T(1024)(128)(4,1)}), s8[1048576]{0:T(1024)(128)(4,1)S(1)}, s32[]{:S(2)}) async-start(s8[9437184]{0:T(1024)(128)(4,1)} %bitcast.153), calls=%async_computation.15 | async-start | bytes 2097152
  1185.6 55.5 %copy-start.4 = (bf16[256,1536]{1,0:T(8,128)(2,1)S(1)}, bf16[256,1536]{1,0:T(8,128)(2,1)}, u32[]{:S(2)}) copy-start(bf16[256,1536]{1,0:T(8,128)(2,1)} %param.11) | copy-start | bytes 2359300
  1185.6 55.5 %copy-start.16 = (bf16[256,1536]{0,1:T(8,128)(2,1)S(1)}, bf16[256,1536]{0,1:T(8,128)(2,1)}, u32[]{:S(2)}) copy-start(bf16[256,1536]{0,1:T(8,128)(2,1)} %copy-done.15) | copy-start | bytes 2359300
  1185.6 55.5 %copy-start.29 = (bf16[8,96,256]{2,1,0:T(8,128)(2,1)S(1)}, bf16[8,96,256]{2,1,0:T(8,128)(2,1)}, u32[]{:S(2)}) copy-start(bf16[8,96,256]{2,1,0:T(8,128)(2,1)} %copy-done.28) | copy-start | bytes 1179652
  1185.6 55.6 %copy-start.35 = (f32[256]{0:T(256)S(1)}, f32[256]{0:T(256)}, u32[]{:S(2)}) copy-start(f32[256]{0:T(256)} %copy-done.33) | copy-start | bytes 3076
  1245.9 28.2 %copy-start.38 = (f32[256]{0:T(256)S(1)}, f32[256]{0:T(256)}, u32[]{:S(2)}) copy-start(f32[256]{0:T(256)} %compare_convert_fusion) | copy-start | bytes 3076
  1268.9 5.1 copy-start.10
  1431.2 9.3 copy-start.14
  1440.5 3.6 copy-start.17
  1444.1 2.8 copy-start.23
  (12 other events, 14.8 us)
Sparse Core Ops, SparseCore 0:
  9.8 98.9 all-gather.10
  110.6 56.9 all-gather.12
  169.5 227.5 all-gather.14
  398.8 122.4 all-gather.16
  552.2 58.4 reduce-scatter.6
  613.7 171.8 reduce-scatter.4
  789.3 152.0 reduce-scatter.10
  944.4 221.6 reduce-scatter.8
  1168.8 262.3 all-reduce.6
